TPU v7x, 32 devices: a whole 2x2x4 slice. The times are simulated.
32 devices in a mesh: rows: 8 (over y, x, core), model: 4 (over z).
Axes of the slice: x: 2, y: 2, z: 4, core: 2. Of those that a mesh axis runs over, the one named last changes fastest.
Arguments:
- one_query: float32 [5120, 5120], P('rows', 'model'), may hold values from -0.125 to 0.125
- other_query: float32 [5120, 5120], P('rows', 'model'), may hold values from -0.078125 to 0.078125
- one_key: float32 [5120, 5120], P('rows', 'model'), may hold values from -0.125 to 0.125
- other_key: float32 [5120, 5120], P('rows', 'model'), may hold values from -0.078125 to 0.078125
- one_value: float32 [5120, 5120], P('rows', 'model'), may hold values from -0.125 to 0.125
- other_value: float32 [5120, 5120], P('rows', 'model'), may hold values from -0.078125 to 0.078125
- mix_share: float32 [5120], P('rows'), may hold values from 0.2 to 0.8
- norm_gain: float32 [5120], P('rows'), may hold values from 0.25 to 1.75
Outputs:
- final_query: bfloat16 [5120, 5120], P(None, 'model')
- final_key: bfloat16 [5120, 5120], P(None, 'model')
- final_value: bfloat16 [5120, 5120], P(None, 'model')
- factor_query: float32 [5120], P('model')
- factor_key: float32 [5120], P('model')
- factor_value: float32 [5120], P('model')
All inputs are finite; a program needn't handle non-finite values. Where the computation divides by a largest or mean magnitude, that divisor is 1e-20 or more.
Results may differ from a plain program's by a relative error of at most 0.001.
Values may be sent and summed in bfloat16 or wider, within the bound.
A program may use at most 192 MiB of HBM per device.

v0:
```python
import functools

import jax
import jax.numpy as jnp
from jax import lax
from jax.experimental import pallas as pl
from jax.experimental.pallas import tpu as pltpu
from jax.sharding import PartitionSpec as P

MESH = pl.DeviceIdType.MESH
LANES = 128
OWN_X, OWN_Y, OWN_S, DIAG, X_S, Y_S, D_S = range(7)


def gathered_by_collectives(one_query, other_query, one_key, other_key, one_value, other_value, mix_share, norm_gain):
    share, gain = mix_share[:, None], norm_gain[:, None]
    gained = [
        (share * one + (1.0 - share) * other) * gain
        for one, other in ((one_query, other_query), (one_key, other_key), (one_value, other_value))
    ]
    factors = lax.pmax(tuple(jnp.max(jnp.abs(g), axis=0) for g in gained), "rows")
    narrow = [(g / f).astype(jnp.bfloat16) for g, f in zip(gained, factors)]
    return (*(lax.all_gather(w, "rows", axis=0, tiled=True) for w in narrow), *factors)


def opposite(me, d):
    core, east, north = lax.rem(me, 2), lax.rem(me // 2, 2), me // 4
    return (
        lax.rem(north + d // 4, 2) * 4
        + lax.rem(east + (d // 2) % 2, 2) * 2
        + lax.rem(core + d % 2, 2)
    )


def parts_of(columns):
    first = 2 * LANES
    return (
        (0, 0, first, 4),
        (0, first, columns - first, 4),
        (1, 0, columns, 8),
        (2, 0, columns, 8),
    )


def late_pairs(parts, p):
    return {len(parts) - 2: 1, len(parts) - 1: parts[p][3] // 2}.get(p, 0)


def kernel(parts, share, gain, *refs):
    args, factors, gathered, late = refs[0:6], *refs[6:9]
    (held, wide_one, wide_other, box_first, box_next, box_rest,
     load_sem, send_sem, bulk_sem, own_sem, d_sem, box_sem, late_sem) = refs[9:]
    rows = args[0].shape[0]
    every = range(len(parts))

    me = lax.axis_index("rows")
    core = lax.rem(me, 2)
    sibling, at_x, at_y, at_d = (opposite(me, d) for d in (1, 2, 4, 6))
    near = at_x + core * (at_y - at_x)
    side = at_y + core * (at_x - at_y)

    def columns_of(p):
        return pl.ds(parts[p][1], parts[p][2])

    def load(p):
        m = parts[p][0]
        for i in (2 * m, 2 * m + 1):
            pltpu.make_async_copy(
                args[i].at[:, columns_of(p)], held.at[i, :, columns_of(p)], load_sem.at[p]
            ).start()

    def loaded(p):
        ref = held.at[pl.ds(2 * parts[p][0], 2), :, columns_of(p)]
        pltpu.make_async_copy(ref, ref, load_sem.at[p]).wait()

    load(0)

    barrier = pltpu.get_barrier_semaphore()
    for d in range(1, 8):
        pl.semaphore_signal(barrier, inc=1, device_id={"rows": opposite(me, d)}, device_id_type=MESH)

    for j in range(rows // LANES):
        s = jnp.broadcast_to(share[j * LANES:(j + 1) * LANES][None], (LANES, LANES)).T
        g = jnp.broadcast_to(gain[j * LANES:(j + 1) * LANES][None], (LANES, LANES)).T
        wide_one[j * LANES:(j + 1) * LANES, :] = s * g
        wide_other[j * LANES:(j + 1) * LANES, :] = (1.0 - s) * g

    def mix(p):
        m, _, width, _ = parts[p]

        def body(i, top):
            at = pl.ds(pl.multiple_of(i * 8, 8), 8)
            a = jnp.concatenate([wide_one[at, :]] * (width // LANES), axis=1)
            b = jnp.concatenate([wide_other[at, :]] * (width // LANES), axis=1)
            mixed = a * held[2 * m, at, columns_of(p)] + b * held[2 * m + 1, at, columns_of(p)]
            held[2 * m, at, columns_of(p)] = mixed
            return jnp.maximum(top, jnp.abs(mixed))

        top = lax.fori_loop(0, rows // 8, body, jnp.zeros((8, width), jnp.float32), unroll=4)
        return jnp.max(top, axis=0, keepdims=True)

    def exchange(box, which):
        for d in range(1, 8):
            pltpu.make_async_remote_copy(
                box.at[me], box.at[me], box_sem.at[2 * which], box_sem.at[2 * which + 1],
                device_id={"rows": opposite(me, d)}, device_id_type=MESH,
            ).start()

    def exchanged(box, which):
        return pltpu.make_async_remote_copy(
            box.at[pl.ds(0, 7)], box.at[pl.ds(0, 7)], box_sem.at[2 * which], box_sem.at[2 * which + 1],
            device_id={"rows": sibling}, device_id_type=MESH,
        )

    def height(p):
        return rows // parts[p][3]

    def piece(p, owner, k, count=1):
        at = pl.multiple_of(owner * rows + k * height(p), 16)
        return gathered.at[parts[p][0], pl.ds(at, count * height(p)), columns_of(p)]

    def send(p, owner, k, stream, target, arrive):
        ref = piece(p, owner, k)
        pltpu.make_async_remote_copy(
            ref, ref, send_sem.at[stream], arrive, device_id={"rows": target}, device_id_type=MESH
        ).start()

    def arrived(ref, arrive, stream=0):
        return pltpu.make_async_remote_copy(
            ref, ref, send_sem.at[stream], arrive, device_id={"rows": sibling}, device_id_type=MESH
        )

    def narrow(p, k, inverse):
        m = parts[p][0]

        def body(i, _):
            at = pl.multiple_of(k * height(p) + i * 16, 16)
            small = (held[2 * m, pl.ds(at, 16), columns_of(p)] * inverse).astype(jnp.bfloat16)
            gathered[m, pl.ds(pl.multiple_of(me * rows + at, 16), 16), columns_of(p)] = small
            return 0

        lax.fori_loop(0, height(p) // 16, body, 0, unroll=True)

    def send_own(p, k):
        send(p, me, k, OWN_X, at_x, own_sem.at[p, k])
        send(p, me, k, OWN_Y, at_y, own_sem.at[p, k])
        send(p, me, k, OWN_S, sibling, bulk_sem.at[OWN_S])

    def narrow_and_send(p, factor, sent):
        factors[parts[p][0], :, columns_of(p)] = factor
        inverse = 1.0 / factor
        for k in range(parts[p][3]):
            narrow(p, k, inverse)
            if 1 <= k <= sent:
                send_own(p, k - 1)
        if sent == parts[p][3]:
            send_own(p, sent - 1)

    loaded(0)
    load(1)
    box_first[me] = mix(0)
    pl.semaphore_wait(barrier, 7)
    exchange(box_first, 0)
    exchanged(box_first, 0).wait_recv()
    narrow_and_send(0, jnp.max(box_first[...], axis=0), 1)
    loaded(1)
    load(2)
    load(3)
    box_next[me] = mix(1)
    exchange(box_next, 1)
    for k in range(1, parts[0][3]):
        send_own(0, k)
    exchanged(box_next, 1).wait_recv()
    narrow_and_send(1, jnp.max(box_next[...], axis=0), parts[1][3] // 2)
    loaded(2)
    box_rest[me, 0:1] = mix(2)
    loaded(3)
    box_rest[me, 1:2] = mix(3)
    exchange(box_rest, 2)
    for k in range(parts[1][3] // 2, parts[1][3]):
        send_own(1, k)
    exchanged(box_rest, 2).wait_recv()
    both = jnp.max(box_rest[...], axis=0)
    for p in (2, 3):
        narrow_and_send(p, both[p - 2:p - 1], parts[p][3])

    aside = 0
    for p in every:
        chunks = parts[p][3]
        half = chunks // 2
        for k in range(chunks):
            arrived(piece(p, 0, 0, 2), own_sem.at[p, k]).wait_recv()
            send(p, at_x, k, X_S, sibling, bulk_sem.at[X_S])
            send(p, at_y, k, Y_S, sibling, bulk_sem.at[Y_S])
            j = k % half
            if j >= late_pairs(parts, p):
                if k < half:
                    send(p, at_x, k, DIAG, at_y, d_sem.at[p, j])
                else:
                    send(p, at_y, k, DIAG, at_x, d_sem.at[p, j])
            elif k >= half:
                send(p, near, j + core * half, DIAG, side, d_sem.at[p, j])
                pltpu.make_async_copy(
                    piece(p, side, j + (1 - core) * half),
                    late.at[pl.ds(aside, height(p)), :],
                    late_sem,
                ).start()
                aside += height(p)
    for p in every:
        half = parts[p][3] // 2
        for j in range(half):
            if j >= late_pairs(parts, p):
                arrived(piece(p, 0, 0, 2), d_sem.at[p, j]).wait_recv()
                send(p, at_d, j, D_S, sibling, bulk_sem.at[D_S])
                send(p, at_d, j + half, D_S, sibling, bulk_sem.at[D_S])
            else:
                arrived(piece(p, 0, 0, 1), d_sem.at[p, j]).wait_recv()
                send(p, at_d, j + core * half, D_S, sibling, bulk_sem.at[D_S])

    matrices = gathered.at[:, pl.ds(0, rows), :]
    relayed = gathered.at[0, pl.ds(0, 3 * rows - late.shape[0]), :]
    for stream in range(7):
        moved = arrived(relayed if stream in (DIAG, D_S) else matrices, bulk_sem.at[stream], stream)
        if stream in (OWN_S, X_S, Y_S, D_S):
            moved.wait_recv()
        moved.wait_send()
    pltpu.make_async_copy(gathered.at[0, pl.ds(0, late.shape[0]), :], late, late_sem).wait()
    for which, box in enumerate((box_first, box_next, box_rest)):
        exchanged(box, which).wait_send()


def settle(parts, factors, gathered, *refs):
    targets, sems = refs[:6], refs[6]
    rows = gathered.shape[1] // 8
    me = lax.axis_index("rows")
    copies = []

    def write(m, at, size):
        at = pl.multiple_of(at, 16)
        copies.append(
            pltpu.make_async_copy(
                gathered.at[m, pl.ds(at, size), :], targets[m].at[pl.ds(at, size), :], sems.at[len(copies)]
            )
        )

    for p in range(len(parts) - 3, len(parts)):
        m, _, _, chunks = parts[p]
        height, half = rows // chunks, chunks // 2
        for d in range(8):
            owner = opposite(me, d)
            core = lax.rem(owner, 2)
            late = late_pairs(parts, p)
            if late == 0 or d < 6:
                write(m, owner * rows, rows)
            elif late == half:
                write(m, owner * rows + core * half * height, half * height)
            else:
                write(m, owner * rows + core * late * height, half * height)
                write(m, owner * rows + (half + late) * height, (half - late) * height)
    for c in copies:
        c.start()
    for m in range(3):
        targets[3 + m][...] = factors[m, 0]
    for c in copies:
        c.wait()


def finish(parts, mine, other, key, value, out_key, out_value, sems):
    rows = value.shape[0] // 8
    me = lax.axis_index("rows")
    copies = []
    for d, late in ((6, mine), (7, other)):
        owner = opposite(me, d)
        core = lax.rem(owner, 2)
        start = 0
        for p, out in ((len(parts) - 2, out_key), (len(parts) - 1, out_value)):
            chunks = parts[p][3]
            size = rows // chunks * late_pairs(parts, p)
            at = pl.multiple_of(owner * rows + (1 - core) * (rows // 2), 16)
            copies.append(
                pltpu.make_async_copy(
                    late.at[pl.ds(start, size), :], out.at[pl.ds(at, size), :], sems.at[len(copies)]
                )
            )
            start += size
    for c in copies:
        c.start()
    for c in copies:
        c.wait()


def gathered_by_kernel(*arrays):
    *weights, mix_share, norm_gain = arrays
    rows, columns = weights[0].shape
    parts = parts_of(columns)
    most = max(part[3] for part in parts)
    late_rows = sum(rows // part[3] * late_pairs(parts, p) for p, part in enumerate(parts))
    vmem, hbm = pl.BlockSpec(memory_space=pltpu.VMEM), pl.BlockSpec(memory_space=pltpu.HBM)
    anywhere = pl.BlockSpec(memory_space=pl.ANY)
    dma = pltpu.SemaphoreType.DMA
    results = pl.pallas_call(
        functools.partial(kernel, parts),
        out_shape=[
            pltpu.VMEM((3, 1, columns), jnp.float32),
            pltpu.VMEM((3, 8 * rows, columns), jnp.bfloat16),
            pltpu.VMEM((late_rows, columns), jnp.bfloat16),
        ],
        in_specs=[vmem] * 2 + [hbm] * 6,
        out_specs=[vmem] * 3,
        scratch_shapes=[
            pltpu.VMEM((6, rows, columns), jnp.float32),
            pltpu.VMEM((rows, LANES), jnp.float32),
            pltpu.VMEM((rows, LANES), jnp.float32),
            pltpu.VMEM((8, 1, parts[0][2]), jnp.float32),
            pltpu.VMEM((8, 1, parts[1][2]), jnp.float32),
            pltpu.VMEM((8, 2, columns), jnp.float32),
            dma((4,)),
            dma((7,)),
            dma((7,)),
            dma((4, most)),
            dma((4, most // 2)),
            dma((6,)),
            dma(()),
        ],
        compiler_params=pltpu.CompilerParams(
            collective_id=0, has_side_effects=True, vmem_limit_bytes=21 * 2**20
        ),
    )(mix_share, norm_gain, *weights)
    factors, gathered, late = [pltpu.with_memory_space_constraint(r, pltpu.VMEM) for r in results]
    whole = jax.ShapeDtypeStruct((8 * rows, columns), jnp.bfloat16)
    mine = lax.ppermute(late, "rows", [(i, i ^ (2, 4)[i % 2]) for i in range(8)])
    query, key, value, *factors = pl.pallas_call(
        functools.partial(settle, parts),
        out_shape=[whole] * 3 + [jax.ShapeDtypeStruct((columns,), jnp.float32)] * 3,
        in_specs=[vmem] * 2,
        out_specs=[anywhere] * 3 + [vmem] * 3,
        scratch_shapes=[dma((26,))],
        cost_estimate=pl.CostEstimate(flops=0, bytes_accessed=48 * rows * columns, transcendentals=0),
        compiler_params=pltpu.CompilerParams(vmem_limit_bytes=2**20),
    )(factors, gathered)
    mine, key, value = lax.optimization_barrier((mine, key, value))
    other = lax.ppermute(mine, "rows", [(i, i ^ 1) for i in range(8)])
    key, value = pl.pallas_call(
        functools.partial(finish, parts),
        out_shape=[whole] * 2,
        in_specs=[vmem] * 2 + [anywhere] * 2,
        out_specs=[anywhere] * 2,
        scratch_shapes=[dma((4,))],
        input_output_aliases={2: 0, 3: 1},
        compiler_params=pltpu.CompilerParams(vmem_limit_bytes=2**20),
    )(mine, other, key, value)
    return query, key, value, *factors


def solution(mesh):
    placed = (P("rows", "model"),) * 6 + (P("rows"),) * 2
    local = gathered_by_kernel if mesh.shape["rows"] == 8 else gathered_by_collectives
    return jax.shard_map(
        local,
        mesh=mesh,
        in_specs=placed,
        out_specs=(P(None, "model"),) * 3 + (P("model"),) * 3,
        check_vma=False,
    )
```

profile of v0, /device:TPU:0, one launch (start us, length us, event | category | flops | bytes accessed | tf_op | source)
XLA Modules:
  0.0 178.7 jit_solution(5606842292812936243)
XLA Ops:
  0.6 159.5 %shard_map.127 = (f32[3,1,1280]{2,1,0:T(1,128)S(1)}, bf16[3,5120,1280]{2,1,0:T(8,128)(2,1)S(1)}, bf16[400,1280]{1,0:T(8,128)(2,1)S(1)}) custom-call(f32[640]{0:T(1024)} %share.1, f32[640]{0:T(1024)} %gain.1, f32[640,1280]{1,0:T(8,128)} %refs_0_.1, f32[640,1280]{1,0:T(8,128)} %refs_1_.1, f32[640,1280]{1,0:T(8,128)} %refs_2_.1, f32[640,1280]{1,0:T(8,128)} %refs_3_.1, ...), custom_call_target="tpu_custom_call" | custom-call | tf_op jit(solution)/shard_map/pallas_call | solution.py:301
  160.1 1.3 collective-permute-start
  161.4 12.8 %shard_map.128 = (bf16[5120,1280]{1,0:T(8,128)(2,1)}, bf16[5120,1280]{1,0:T(8,128)(2,1)}, bf16[5120,1280]{1,0:T(8,128)(2,1)}, f32[1280]{0:T(1024)}, f32[1280]{0:T(1024)}, /*index=5*/f32[1280]{0:T(1024)}) custom-call(f32[3,1,1280]{2,1,0:T(1,128)S(1)} %get-tuple-element.20.factors, bf16[3,5120,1280]{2,1,0:T(8,128)(2,1)S(1)} %get-tuple-element.21.gathered), custom_call_target="tpu_custom_call" | custom-call | bytes 39321600 | tf_op jit(solution)/shard_map/pallas_call | solution.py:332
  174.2 0.5 collective-permute-done.mine
  174.7 0.0 collective-permute-start.1
  174.7 2.6 %collective-permute-done.1.other = bf16[400,1280]{1,0:T(8,128)(2,1)S(1)} collective-permute-done((bf16[400,1280]{1,0:T(8,128)(2,1)S(1)}, bf16[400,1280]{1,0:T(8,128)(2,1)S(1)}, u32[]{:S(2)}, u32[]{:S(2)}) %collective-permute-start.1) | collective-permute-done | bytes 1024032 | tf_op jit(solution)/shard_map/ppermute | solution.py:342
  177.4 1.3 shard_map.129
Async XLA Ops:
  160.1 14.6 %collective-permute-start = (bf16[400,1280]{1,0:T(8,128)(2,1)S(1)}, bf16[400,1280]{1,0:T(8,128)(2,1)S(1)}, u32[]{:S(2)}, u32[]{:S(2)}) collective-permute-start(bf16[400,1280]{1,0:T(8,128)(2,1)S(1)} %get-tuple-element.23), channel_id=1, source_target_pairs={{0,8},{4,20},{8,0},{12,28},{16,24},{20,4},{24,16},{28,12},{1,9},{5... | collective-permute-start | bytes 3072008 | tf_op jit(solution)/shard_map/ppermute | solution.py:331
  174.7 2.6 %collective-permute-start.1 = (bf16[400,1280]{1,0:T(8,128)(2,1)S(1)}, bf16[400,1280]{1,0:T(8,128)(2,1)S(1)}, u32[]{:S(2)}, u32[]{:S(2)}) collective-permute-start(bf16[400,1280]{1,0:T(8,128)(2,1)S(1)} %collective-permute-done.mine), channel_id=1, source_target_pairs={{0,4},{4,0},{8,12},{12,8},{16,20},{20,16},{24,28},{28,24},{1,5},{5... | collective-permute-start | bytes 3072008 | tf_op jit(solution)/shard_map/ppermute | solution.py:342
where the time goes:
time: 179 us
  Pallas kernels  174 us (97%)
  waiting for transfers between devices  3.11 us (2%)
    pallas_call x1, Pallas kernels, gathered_by_kernel(): pl.pallas_call(functools.partial(kernel, parts), out_shape=[pltpu.VMEM((3...  159 us
    pallas_call x1, Pallas kernels, gathered_by_kernel(): pl.pallas_call(functools.partial(settle, parts), out_shape=[whole] * 3 +...  12.8 us
  transfers between devices with their start and end apart: 2, of which 2 were waited for; matrix products, arithmetic and copies ran while one was open for 0% of the time, Pallas kernels for 7%

commit v1 on v0

--- a/solution.py
+++ b/solution.py
@@ -35,8 +35,8 @@
 def parts_of(columns):
     first = 2 * LANES
     return (
-        (0, 0, first, 4),
-        (0, first, columns - first, 4),
+        (0, 0, first, 10),
+        (0, first, columns - first, 2),
         (1, 0, columns, 8),
         (2, 0, columns, 8),
     )
@@ -48,10 +48,11 @@
 
 def kernel(parts, share, gain, *refs):
     args, factors, gathered, late = refs[0:6], *refs[6:9]
-    (held, wide_one, wide_other, box_first, box_next, box_rest,
-     load_sem, send_sem, bulk_sem, own_sem, d_sem, box_sem, late_sem) = refs[9:]
-    rows = args[0].shape[0]
+    (held, wide_one, wide_other, box_first, box_next, box_rest, early,
+     load_sem, send_sem, bulk_sem, own_sem, d_sem, box_sem, late_sem, early_sem) = refs[9:]
+    rows, columns = args[0].shape
     every = range(len(parts))
+    base = [sum(part[3] for part in parts[:p]) for p in every]
 
     me = lax.axis_index("rows")
     core = lax.rem(me, 2)
@@ -100,7 +101,7 @@
         return jnp.max(top, axis=0, keepdims=True)
 
     def exchange(box, which):
-        for d in range(1, 8):
+        for d in (6, 7, 2, 4, 3, 5, 1):
             pltpu.make_async_remote_copy(
                 box.at[me], box.at[me], box_sem.at[2 * which], box_sem.at[2 * which + 1],
                 device_id={"rows": opposite(me, d)}, device_id_type=MESH,
@@ -142,8 +143,9 @@
         lax.fori_loop(0, height(p) // 16, body, 0, unroll=True)
 
     def send_own(p, k):
-        send(p, me, k, OWN_X, at_x, own_sem.at[p, k])
-        send(p, me, k, OWN_Y, at_y, own_sem.at[p, k])
+        if p or k not in ahead:
+            send(p, me, k, OWN_X, at_x, own_sem.at[base[p] + k])
+            send(p, me, k, OWN_Y, at_y, own_sem.at[base[p] + k])
         send(p, me, k, OWN_S, sibling, bulk_sem.at[OWN_S])
 
     def narrow_and_send(p, factor, sent):
@@ -156,20 +158,50 @@
         if sent == parts[p][3]:
             send_own(p, sent - 1)
 
+    ahead = (0, parts[0][3] // 2)
+
+    def send_early():
+        for place, target in enumerate((at_x, at_y)):
+            for i, k in enumerate(ahead):
+                pltpu.make_async_remote_copy(
+                    held.at[0, pl.ds(k * height(0), height(0)), columns_of(0)],
+                    early.at[place, i],
+                    early_sem.at[0],
+                    early_sem.at[1],
+                    device_id={"rows": target},
+                    device_id_type=MESH,
+                ).start()
+
+    early_all = pltpu.make_async_remote_copy(
+        early, early, early_sem.at[0], early_sem.at[1], device_id={"rows": at_x}, device_id_type=MESH
+    )
+
+    def narrow_early():
+        early_all.wait_recv()
+        inverse = 1.0 / factors[0, :, columns_of(0)]
+        for place, owner in enumerate((at_x, at_y)):
+            for i, k in enumerate(ahead):
+                for r in range(0, height(0), 16):
+                    at = pl.multiple_of(owner * rows + k * height(0) + r, 16)
+                    small = (early[place, i, r:r + 16, :] * inverse).astype(jnp.bfloat16)
+                    gathered[0, pl.ds(at, 16), columns_of(0)] = small
+
     loaded(0)
     load(1)
     box_first[me] = mix(0)
     pl.semaphore_wait(barrier, 7)
     exchange(box_first, 0)
+    send_early()
     exchanged(box_first, 0).wait_recv()
-    narrow_and_send(0, jnp.max(box_first[...], axis=0), 1)
+    narrow_and_send(0, jnp.max(box_first[...], axis=0), 3)
     loaded(1)
     load(2)
     load(3)
     box_next[me] = mix(1)
     exchange(box_next, 1)
-    for k in range(1, parts[0][3]):
+    for k in range(3, parts[0][3]):
         send_own(0, k)
+    narrow_early()
     exchanged(box_next, 1).wait_recv()
     narrow_and_send(1, jnp.max(box_next[...], axis=0), parts[1][3] // 2)
     loaded(2)
@@ -189,17 +221,18 @@
         chunks = parts[p][3]
         half = chunks // 2
         for k in range(chunks):
-            arrived(piece(p, 0, 0, 2), own_sem.at[p, k]).wait_recv()
+            if p or k not in ahead:
+                arrived(piece(p, 0, 0, 2), own_sem.at[base[p] + k]).wait_recv()
             send(p, at_x, k, X_S, sibling, bulk_sem.at[X_S])
             send(p, at_y, k, Y_S, sibling, bulk_sem.at[Y_S])
             j = k % half
             if j >= late_pairs(parts, p):
                 if k < half:
-                    send(p, at_x, k, DIAG, at_y, d_sem.at[p, j])
+                    send(p, at_x, k, DIAG, at_y, d_sem.at[base[p] // 2 + j])
                 else:
-                    send(p, at_y, k, DIAG, at_x, d_sem.at[p, j])
+                    send(p, at_y, k, DIAG, at_x, d_sem.at[base[p] // 2 + j])
             elif k >= half:
-                send(p, near, j + core * half, DIAG, side, d_sem.at[p, j])
+                send(p, near, j + core * half, DIAG, side, d_sem.at[base[p] // 2 + j])
                 pltpu.make_async_copy(
                     piece(p, side, j + (1 - core) * half),
                     late.at[pl.ds(aside, height(p)), :],
@@ -210,20 +243,28 @@
         half = parts[p][3] // 2
         for j in range(half):
             if j >= late_pairs(parts, p):
-                arrived(piece(p, 0, 0, 2), d_sem.at[p, j]).wait_recv()
+                arrived(piece(p, 0, 0, 2), d_sem.at[base[p] // 2 + j]).wait_recv()
                 send(p, at_d, j, D_S, sibling, bulk_sem.at[D_S])
                 send(p, at_d, j + half, D_S, sibling, bulk_sem.at[D_S])
             else:
-                arrived(piece(p, 0, 0, 1), d_sem.at[p, j]).wait_recv()
+                arrived(piece(p, 0, 0, 1), d_sem.at[base[p] // 2 + j]).wait_recv()
                 send(p, at_d, j + core * half, D_S, sibling, bulk_sem.at[D_S])
 
-    matrices = gathered.at[:, pl.ds(0, rows), :]
-    relayed = gathered.at[0, pl.ds(0, 3 * rows - late.shape[0]), :]
-    for stream in range(7):
-        moved = arrived(relayed if stream in (DIAG, D_S) else matrices, bulk_sem.at[stream], stream)
+    width = parts[0][2]
+    sizes = {
+        stream: gathered.at[:, pl.ds(0, rows), :] for stream in (OWN_S, X_S, Y_S)
+    } | {
+        stream: gathered.at[0, pl.ds(0, 3 * rows - late.shape[0]), :] for stream in (DIAG, D_S)
+    } | {
+        stream: gathered.at[pl.ds(0, 2), pl.ds(0, 3 * rows * columns // (2 * width) - height(0)), pl.ds(0, width)]
+        for stream in (OWN_X, OWN_Y)
+    }
+    for stream, size in sizes.items():
+        moved = arrived(size, bulk_sem.at[stream], stream)
         if stream in (OWN_S, X_S, Y_S, D_S):
             moved.wait_recv()
         moved.wait_send()
+    early_all.wait_send()
     pltpu.make_async_copy(gathered.at[0, pl.ds(0, late.shape[0]), :], late, late_sem).wait()
     for which, box in enumerate((box_first, box_next, box_rest)):
         exchanged(box, which).wait_send()
@@ -265,24 +306,19 @@
         c.wait()
 
 
-def finish(parts, mine, other, key, value, out_key, out_value, sems):
+def finish(parts, d, late, key, value, out_key, out_value, sems):
     rows = value.shape[0] // 8
-    me = lax.axis_index("rows")
-    copies = []
-    for d, late in ((6, mine), (7, other)):
-        owner = opposite(me, d)
-        core = lax.rem(owner, 2)
-        start = 0
-        for p, out in ((len(parts) - 2, out_key), (len(parts) - 1, out_value)):
-            chunks = parts[p][3]
-            size = rows // chunks * late_pairs(parts, p)
-            at = pl.multiple_of(owner * rows + (1 - core) * (rows // 2), 16)
-            copies.append(
-                pltpu.make_async_copy(
-                    late.at[pl.ds(start, size), :], out.at[pl.ds(at, size), :], sems.at[len(copies)]
-                )
+    owner = opposite(lax.axis_index("rows"), d)
+    at = pl.multiple_of(owner * rows + (1 - lax.rem(owner, 2)) * (rows // 2), 16)
+    copies, start = [], 0
+    for p, out in ((len(parts) - 2, out_key), (len(parts) - 1, out_value)):
+        size = rows // parts[p][3] * late_pairs(parts, p)
+        copies.append(
+            pltpu.make_async_copy(
+                late.at[pl.ds(start, size), :], out.at[pl.ds(at, size), :], sems.at[len(copies)]
             )
-            start += size
+        )
+        start += size
     for c in copies:
         c.start()
     for c in copies:
@@ -293,7 +329,6 @@
     *weights, mix_share, norm_gain = arrays
     rows, columns = weights[0].shape
     parts = parts_of(columns)
-    most = max(part[3] for part in parts)
     late_rows = sum(rows // part[3] * late_pairs(parts, p) for p, part in enumerate(parts))
     vmem, hbm = pl.BlockSpec(memory_space=pltpu.VMEM), pl.BlockSpec(memory_space=pltpu.HBM)
     anywhere = pl.BlockSpec(memory_space=pl.ANY)
@@ -314,13 +349,15 @@
             pltpu.VMEM((8, 1, parts[0][2]), jnp.float32),
             pltpu.VMEM((8, 1, parts[1][2]), jnp.float32),
             pltpu.VMEM((8, 2, columns), jnp.float32),
+            pltpu.VMEM((2, 2, rows // parts[0][3], parts[0][2]), jnp.float32),
             dma((4,)),
             dma((7,)),
             dma((7,)),
-            dma((4, most)),
-            dma((4, most // 2)),
+            dma((sum(part[3] for part in parts),)),
+            dma((sum(part[3] // 2 for part in parts),)),
             dma((6,)),
             dma(()),
+            dma((2,)),
         ],
         compiler_params=pltpu.CompilerParams(
             collective_id=0, has_side_effects=True, vmem_limit_bytes=21 * 2**20
@@ -340,15 +377,17 @@
     )(factors, gathered)
     mine, key, value = lax.optimization_barrier((mine, key, value))
     other = lax.ppermute(mine, "rows", [(i, i ^ 1) for i in range(8)])
-    key, value = pl.pallas_call(
-        functools.partial(finish, parts),
-        out_shape=[whole] * 2,
-        in_specs=[vmem] * 2 + [anywhere] * 2,
-        out_specs=[anywhere] * 2,
-        scratch_shapes=[dma((4,))],
-        input_output_aliases={2: 0, 3: 1},
-        compiler_params=pltpu.CompilerParams(vmem_limit_bytes=2**20),
-    )(mine, other, key, value)
+    for d, late in ((6, mine), (7, other)):
+        key, value = pl.pallas_call(
+            functools.partial(finish, parts, d),
+            out_shape=[whole] * 2,
+            in_specs=[vmem] + [anywhere] * 2,
+            out_specs=[anywhere] * 2,
+            scratch_shapes=[dma((2,))],
+            input_output_aliases={1: 0, 2: 1},
+            cost_estimate=pl.CostEstimate(flops=0, bytes_accessed=4 * late_rows * columns, transcendentals=0),
+            compiler_params=pltpu.CompilerParams(vmem_limit_bytes=2**20),
+        )(late, key, value)
     return query, key, value, *factors
 
 

time: 179 us -> 177 us (0.989)
  transfers between devices with their start and end apart: 2 -> 2, of which waited for: 2 -> 2; matrix products, arithmetic and copies ran while one was open for 0% -> 0% of each run, Pallas kernels for 7% -> 8%
where the time goes in v1:
time: 177 us
  Pallas kernels  173 us (98%)
  waiting for transfers between devices  2.21 us (1%)
    pallas_call x1, Pallas kernels, gathered_by_kernel(): pl.pallas_call(functools.partial(kernel, parts), out_shape=[pltpu.VMEM((3...  158 us
    pallas_call x1, Pallas kernels, gathered_by_kernel(): pl.pallas_call(functools.partial(settle, parts), out_shape=[whole] * 3 +...  12.8 us
  transfers between devices with their start and end apart: 2, of which 2 were waited for; matrix products, arithmetic and copies ran while one was open for 0% of the time, Pallas kernels for 8%

profile of v1, /device:TPU:0, one launch (start us, length us, event | category | flops | bytes accessed | tf_op | source)
XLA Modules:
  0.0 177.0 jit_solution(13482495006626512693)
XLA Ops:
  0.6 158.1 %shard_map.127 = (f32[3,1,1280]{2,1,0:T(1,128)S(1)}, bf16[3,5120,1280]{2,1,0:T(8,128)(2,1)S(1)}, bf16[400,1280]{1,0:T(8,128)(2,1)S(1)}) custom-call(f32[640]{0:T(1024)} %share.1, f32[640]{0:T(1024)} %gain.1, f32[640,1280]{1,0:T(8,128)} %refs_0_.1, f32[640,1280]{1,0:T(8,128)} %refs_1_.1, f32[640,1280]{1,0:T(8,128)} %refs_2_.1, f32[640,1280]{1,0:T(8,128)} %refs_3_.1, ...), custom_call_target="tpu_custom_call" | custom-call | tf_op jit(solution)/shard_map/pallas_call | solution.py:336
  158.8 1.2 collective-permute-start
  160.0 12.8 %shard_map.128 = (bf16[5120,1280]{1,0:T(8,128)(2,1)}, bf16[5120,1280]{1,0:T(8,128)(2,1)}, bf16[5120,1280]{1,0:T(8,128)(2,1)}, f32[1280]{0:T(1024)}, f32[1280]{0:T(1024)}, /*index=5*/f32[1280]{0:T(1024)}) custom-call(f32[3,1,1280]{2,1,0:T(1,128)S(1)} %get-tuple-element.22.factors, bf16[3,5120,1280]{2,1,0:T(8,128)(2,1)S(1)} %get-tuple-element.23.gathered), custom_call_target="tpu_custom_call" | custom-call | bytes 39321600 | tf_op jit(solution)/shard_map/pallas_call | solution.py:369
  172.8 0.6 collective-permute-done.late
  173.4 0.0 collective-permute-start.1
  173.4 1.0 shard_map.129
  174.3 1.6 collective-permute-done.1.late
  176.0 1.0 shard_map.130
Async XLA Ops:
  158.8 14.6 %collective-permute-start = (bf16[400,1280]{1,0:T(8,128)(2,1)S(1)}, bf16[400,1280]{1,0:T(8,128)(2,1)S(1)}, u32[]{:S(2)}, u32[]{:S(2)}) collective-permute-start(bf16[400,1280]{1,0:T(8,128)(2,1)S(1)} %get-tuple-element.25), channel_id=1, source_target_pairs={{0,8},{4,20},{8,0},{12,28},{16,24},{20,4},{24,16},{28,12},{1,9},{5... | collective-permute-start | bytes 3072008 | tf_op jit(solution)/shard_map/ppermute | solution.py:368
  173.4 2.6 %collective-permute-start.1 = (bf16[400,1280]{1,0:T(8,128)(2,1)S(1)}, bf16[400,1280]{1,0:T(8,128)(2,1)S(1)}, u32[]{:S(2)}, u32[]{:S(2)}) collective-permute-start(bf16[400,1280]{1,0:T(8,128)(2,1)S(1)} %collective-permute-done.late), channel_id=1, source_target_pairs={{0,4},{4,0},{8,12},{12,8},{16,20},{20,16},{24,28},{28,24},{1,5},{5... | collective-permute-start | bytes 3072008 | tf_op jit(solution)/shard_map/ppermute | solution.py:379

commit v2 on v1

--- a/solution.py
+++ b/solution.py
@@ -46,10 +46,10 @@
     return {len(parts) - 2: 1, len(parts) - 1: parts[p][3] // 2}.get(p, 0)
 
 
-def kernel(parts, share, gain, *refs):
-    args, factors, gathered, late = refs[0:6], *refs[6:9]
-    (held, wide_one, wide_other, box_first, box_next, box_rest, early,
-     load_sem, send_sem, bulk_sem, own_sem, d_sem, box_sem, late_sem, early_sem) = refs[9:]
+def kernel(parts, *refs):
+    args, factors, gathered, late, closing = refs[0:8], *refs[8:12]
+    (held, share, gain, wide_one, wide_other, box_first, box_next, box_rest, early,
+     load_sem, send_sem, bulk_sem, own_sem, d_sem, box_sem, late_sem, early_sem, row_sem) = refs[12:]
     rows, columns = args[0].shape
     every = range(len(parts))
     base = [sum(part[3] for part in parts[:p]) for p in every]
@@ -74,12 +74,17 @@
         ref = held.at[pl.ds(2 * parts[p][0], 2), :, columns_of(p)]
         pltpu.make_async_copy(ref, ref, load_sem.at[p]).wait()
 
+    by_row = [pltpu.make_async_copy(args[6 + i], to, row_sem.at[i]) for i, to in enumerate((share, gain))]
+    for c in by_row:
+        c.start()
     load(0)
 
     barrier = pltpu.get_barrier_semaphore()
     for d in range(1, 8):
         pl.semaphore_signal(barrier, inc=1, device_id={"rows": opposite(me, d)}, device_id_type=MESH)
 
+    for c in by_row:
+        c.wait()
     for j in range(rows // LANES):
         s = jnp.broadcast_to(share[j * LANES:(j + 1) * LANES][None], (LANES, LANES)).T
         g = jnp.broadcast_to(gain[j * LANES:(j + 1) * LANES][None], (LANES, LANES)).T
@@ -120,10 +125,11 @@
         at = pl.multiple_of(owner * rows + k * height(p), 16)
         return gathered.at[parts[p][0], pl.ds(at, count * height(p)), columns_of(p)]
 
-    def send(p, owner, k, stream, target, arrive):
+    def send(p, owner, k, stream, target, arrive, to=None):
         ref = piece(p, owner, k)
         pltpu.make_async_remote_copy(
-            ref, ref, send_sem.at[stream], arrive, device_id={"rows": target}, device_id_type=MESH
+            ref, ref if to is None else to, send_sem.at[stream], arrive,
+            device_id={"rows": target}, device_id_type=MESH,
         ).start()
 
     def arrived(ref, arrive, stream=0):
@@ -216,6 +222,9 @@
     for p in (2, 3):
         narrow_and_send(p, both[p - 2:p - 1], parts[p][3])
 
+    def closes(p, j):
+        return p == every[-1] and j == parts[p][3] // 2 - 1
+
     aside = 0
     for p in every:
         chunks = parts[p][3]
@@ -232,7 +241,10 @@
                 else:
                     send(p, at_y, k, DIAG, at_x, d_sem.at[base[p] // 2 + j])
             elif k >= half:
-                send(p, near, j + core * half, DIAG, side, d_sem.at[base[p] // 2 + j])
+                send(
+                    p, near, j + core * half, DIAG, side, d_sem.at[base[p] // 2 + j],
+                    closing if closes(p, j) else None,
+                )
                 pltpu.make_async_copy(
                     piece(p, side, j + (1 - core) * half),
                     late.at[pl.ds(aside, height(p)), :],
@@ -248,13 +260,15 @@
                 send(p, at_d, j + half, D_S, sibling, bulk_sem.at[D_S])
             else:
                 arrived(piece(p, 0, 0, 1), d_sem.at[base[p] // 2 + j]).wait_recv()
-                send(p, at_d, j + core * half, D_S, sibling, bulk_sem.at[D_S])
+                if not closes(p, j):
+                    send(p, at_d, j + core * half, D_S, sibling, bulk_sem.at[D_S])
 
     width = parts[0][2]
     sizes = {
         stream: gathered.at[:, pl.ds(0, rows), :] for stream in (OWN_S, X_S, Y_S)
     } | {
-        stream: gathered.at[0, pl.ds(0, 3 * rows - late.shape[0]), :] for stream in (DIAG, D_S)
+        DIAG: gathered.at[0, pl.ds(0, 3 * rows - late.shape[0]), :],
+        D_S: gathered.at[0, pl.ds(0, 3 * rows - late.shape[0] - closing.shape[0]), :],
     } | {
         stream: gathered.at[pl.ds(0, 2), pl.ds(0, 3 * rows * columns // (2 * width) - height(0)), pl.ds(0, width)]
         for stream in (OWN_X, OWN_Y)
@@ -294,7 +308,7 @@
             if late == 0 or d < 6:
                 write(m, owner * rows, rows)
             elif late == half:
-                write(m, owner * rows + core * half * height, half * height)
+                write(m, owner * rows + core * half * height, (half - 1) * height)
             else:
                 write(m, owner * rows + core * late * height, half * height)
                 write(m, owner * rows + (half + late) * height, (half - late) * height)
@@ -306,19 +320,31 @@
         c.wait()
 
 
-def finish(parts, d, late, key, value, out_key, out_value, sems):
+def finish(parts, places, *refs):
+    given = refs[:len(places)]
+    key, value, sems = refs[-3:]
     rows = value.shape[0] // 8
-    owner = opposite(lax.axis_index("rows"), d)
-    at = pl.multiple_of(owner * rows + (1 - lax.rem(owner, 2)) * (rows // 2), 16)
-    copies, start = [], 0
-    for p, out in ((len(parts) - 2, out_key), (len(parts) - 1, out_value)):
-        size = rows // parts[p][3] * late_pairs(parts, p)
+    copies = []
+
+    def write(ref, start, size, out, at):
+        at = pl.multiple_of(at, 16)
         copies.append(
             pltpu.make_async_copy(
-                late.at[pl.ds(start, size), :], out.at[pl.ds(at, size), :], sems.at[len(copies)]
+                ref.at[pl.ds(start, size), :], out.at[pl.ds(at, size), :], sems.at[len(copies)]
             )
         )
-        start += size
+
+    for ref, (closing, d) in zip(given, places):
+        owner = opposite(lax.axis_index("rows"), d)
+        core = lax.rem(owner, 2)
+        if closing:
+            write(ref, 0, ref.shape[0], value, owner * rows + (1 + core) * (rows // 2) - ref.shape[0])
+            continue
+        start = 0
+        for p, out in ((len(parts) - 2, key), (len(parts) - 1, value)):
+            size = rows // parts[p][3] * late_pairs(parts, p)
+            write(ref, start, size, out, owner * rows + (1 - core) * (rows // 2))
+            start += size
     for c in copies:
         c.start()
     for c in copies:
@@ -326,8 +352,7 @@
 
 
 def gathered_by_kernel(*arrays):
-    *weights, mix_share, norm_gain = arrays
-    rows, columns = weights[0].shape
+    rows, columns = arrays[0].shape
     parts = parts_of(columns)
     late_rows = sum(rows // part[3] * late_pairs(parts, p) for p, part in enumerate(parts))
     vmem, hbm = pl.BlockSpec(memory_space=pltpu.VMEM), pl.BlockSpec(memory_space=pltpu.HBM)
@@ -339,11 +364,14 @@
             pltpu.VMEM((3, 1, columns), jnp.float32),
             pltpu.VMEM((3, 8 * rows, columns), jnp.bfloat16),
             pltpu.VMEM((late_rows, columns), jnp.bfloat16),
+            pltpu.VMEM((rows // parts[-1][3], columns), jnp.bfloat16),
         ],
-        in_specs=[vmem] * 2 + [hbm] * 6,
-        out_specs=[vmem] * 3,
+        in_specs=[hbm] * 8,
+        out_specs=[vmem] * 4,
         scratch_shapes=[
             pltpu.VMEM((6, rows, columns), jnp.float32),
+            pltpu.VMEM((rows,), jnp.float32),
+            pltpu.VMEM((rows,), jnp.float32),
             pltpu.VMEM((rows, LANES), jnp.float32),
             pltpu.VMEM((rows, LANES), jnp.float32),
             pltpu.VMEM((8, 1, parts[0][2]), jnp.float32),
@@ -358,14 +386,19 @@
             dma((6,)),
             dma(()),
             dma((2,)),
+            dma((2,)),
         ],
         compiler_params=pltpu.CompilerParams(
             collective_id=0, has_side_effects=True, vmem_limit_bytes=21 * 2**20
         ),
-    )(mix_share, norm_gain, *weights)
-    factors, gathered, late = [pltpu.with_memory_space_constraint(r, pltpu.VMEM) for r in results]
+    )(*arrays)
+    factors, gathered, late, closing = [
+        pltpu.with_memory_space_constraint(r, pltpu.VMEM) for r in results
+    ]
     whole = jax.ShapeDtypeStruct((8 * rows, columns), jnp.bfloat16)
+    siblings = [(i, i ^ 1) for i in range(8)]
     mine = lax.ppermute(late, "rows", [(i, i ^ (2, 4)[i % 2]) for i in range(8)])
+    closing_other = lax.ppermute(closing, "rows", siblings)
     query, key, value, *factors = pl.pallas_call(
         functools.partial(settle, parts),
         out_shape=[whole] * 3 + [jax.ShapeDtypeStruct((columns,), jnp.float32)] * 3,
@@ -375,19 +408,23 @@
         cost_estimate=pl.CostEstimate(flops=0, bytes_accessed=48 * rows * columns, transcendentals=0),
         compiler_params=pltpu.CompilerParams(vmem_limit_bytes=2**20),
     )(factors, gathered)
-    mine, key, value = lax.optimization_barrier((mine, key, value))
-    other = lax.ppermute(mine, "rows", [(i, i ^ 1) for i in range(8)])
-    for d, late in ((6, mine), (7, other)):
+    mine, closing_other, key, value = lax.optimization_barrier((mine, closing_other, key, value))
+    other = lax.ppermute(mine, "rows", siblings)
+    for places, given in (
+        (((False, 6), (True, 6), (True, 7)), (mine, closing, closing_other)),
+        (((False, 7),), (other,)),
+    ):
+        n = len(given)
         key, value = pl.pallas_call(
-            functools.partial(finish, parts, d),
+            functools.partial(finish, parts, places),
             out_shape=[whole] * 2,
-            in_specs=[vmem] + [anywhere] * 2,
+            in_specs=[vmem] * n + [anywhere] * 2,
             out_specs=[anywhere] * 2,
-            scratch_shapes=[dma((2,))],
-            input_output_aliases={1: 0, 2: 1},
+            scratch_shapes=[dma((n + 1,))],
+            input_output_aliases={n: 0, n + 1: 1},
             cost_estimate=pl.CostEstimate(flops=0, bytes_accessed=4 * late_rows * columns, transcendentals=0),
             compiler_params=pltpu.CompilerParams(vmem_limit_bytes=2**20),
-        )(late, key, value)
+        )(*given, key, value)
     return query, key, value, *factors
 
 

time: 177 us -> 175 us (0.989)
  Pallas kernels: 173 us -> 171 us
  transfers between devices with their start and end apart: 2 -> 3, of which waited for: 2 -> 2; matrix products, arithmetic and copies ran while one was open for 0% -> 0% of each run, Pallas kernels for 8% -> 8%
where the time goes in v2:
time: 175 us
  Pallas kernels  171 us (98%)
  waiting for transfers between devices  2.15 us (1%)
    pallas_call x1, Pallas kernels, gathered_by_kernel(): pl.pallas_call(functools.partial(kernel, parts), out_shape=[pltpu.VMEM((3...  156 us
    pallas_call x1, Pallas kernels, gathered_by_kernel(): pl.pallas_call(functools.partial(settle, parts), out_shape=[whole] * 3 +...  12.7 us
  transfers between devices with their start and end apart: 3, of which 2 were waited for; matrix products, arithmetic and copies ran while one was open for 0% of the time, Pallas kernels for 8%

profile of v2, /device:TPU:0, one launch (start us, length us, event | category | flops | bytes accessed | tf_op | source)
XLA Modules:
  0.0 175.3 jit_solution(8335307535731189448)
XLA Ops:
  0.6 156.4 %shard_map.127 = (f32[3,1,1280]{2,1,0:T(1,128)S(1)}, bf16[3,5120,1280]{2,1,0:T(8,128)(2,1)S(1)}, bf16[400,1280]{1,0:T(8,128)(2,1)S(1)}, bf16[80,1280]{1,0:T(8,128)(2,1)S(1)}) custom-call(f32[640,1280]{1,0:T(8,128)} %refs_0_.1, f32[640,1280]{1,0:T(8,128)} %refs_1_.1, f32[640,1280]{1,0:T(8,128)} %refs_2_.1, f32[640,1280]{1,0:T(8,128)} %refs_3_.1, ...), custom_call_target="tpu_custom_call" | custom-call | tf_op jit(solution)/shard_map/pallas_call | solution.py:361
  157.1 1.2 collective-permute-start
  158.3 0.0 collective-permute-start.1
  158.3 12.7 %shard_map.128 = (bf16[5120,1280]{1,0:T(8,128)(2,1)}, bf16[5120,1280]{1,0:T(8,128)(2,1)}, bf16[5120,1280]{1,0:T(8,128)(2,1)}, f32[1280]{0:T(1024)}, f32[1280]{0:T(1024)}, /*index=5*/f32[1280]{0:T(1024)}) custom-call(f32[3,1,1280]{2,1,0:T(1,128)S(1)} %get-tuple-element.24.factors, bf16[3,5120,1280]{2,1,0:T(8,128)(2,1)S(1)} %get-tuple-element.25.gathered), custom_call_target="tpu_custom_call" | custom-call | bytes 39321600 | tf_op jit(solution)/shard_map/pallas_call | solution.py:402
  171.0 0.0 collective-permute-done.1.refs_2_
  171.0 0.7 collective-permute-done.refs_0_
  171.7 0.0 collective-permute-start.2
  171.7 1.1 shard_map.129
  172.8 1.5 collective-permute-done.2.refs_0_
  174.3 1.0 shard_map.130
Async XLA Ops:
  157.1 14.6 %collective-permute-start = (bf16[400,1280]{1,0:T(8,128)(2,1)S(1)}, bf16[400,1280]{1,0:T(8,128)(2,1)S(1)}, u32[]{:S(2)}, u32[]{:S(2)}) collective-permute-start(bf16[400,1280]{1,0:T(8,128)(2,1)S(1)} %get-tuple-element.27), channel_id=1, source_target_pairs={{0,8},{4,20},{8,0},{12,28},{16,24},{20,4},{24,16},{28,12},{1,9},{5... | collective-permute-start | bytes 3072008 | tf_op jit(solution)/shard_map/ppermute | solution.py:400
  158.3 12.7 %collective-permute-start.1 = (bf16[80,1280]{1,0:T(8,128)(2,1)S(1)}, bf16[80,1280]{1,0:T(8,128)(2,1)S(1)}, u32[]{:S(2)}, u32[]{:S(2)}) collective-permute-start(bf16[80,1280]{1,0:T(8,128)(2,1)S(1)} %get-tuple-element.28.refs_1_), channel_id=1, source_target_pairs={{0,4},{4,0},{8,12},{12,8},{16,20},{20,16},{24,28},{28,24},{1,5},{5... | collective-permute-start | bytes 614408 | tf_op jit(solution)/shard_map/ppermute | solution.py:401
  171.7 2.6 %collective-permute-start.2 = (bf16[400,1280]{1,0:T(8,128)(2,1)S(1)}, bf16[400,1280]{1,0:T(8,128)(2,1)S(1)}, u32[]{:S(2)}, u32[]{:S(2)}) collective-permute-start(bf16[400,1280]{1,0:T(8,128)(2,1)S(1)} %collective-permute-done.refs_0_), channel_id=1, source_target_pairs={{0,4},{4,0},{8,12},{12,8},{16,20},{20,16},{24,28},{28,24},{1,5},{5... | collective-permute-start | bytes 3072008 | tf_op jit(solution)/shard_map/ppermute | solution.py:412

commit v3 on v2

--- a/solution.py
+++ b/solution.py
@@ -6,6 +6,7 @@
 from jax.experimental import pallas as pl
 from jax.experimental.pallas import tpu as pltpu
 from jax.sharding import PartitionSpec as P
+
 
 MESH = pl.DeviceIdType.MESH
 LANES = 128
@@ -37,21 +38,22 @@
     return (
         (0, 0, first, 10),
         (0, first, columns - first, 2),
-        (1, 0, columns, 8),
-        (2, 0, columns, 8),
+        (1, 0, columns, 10),
+        (2, 0, columns, 10),
     )
 
 
 def late_pairs(parts, p):
-    return {len(parts) - 2: 1, len(parts) - 1: parts[p][3] // 2}.get(p, 0)
+    return {len(parts) - 2: 3, len(parts) - 1: parts[p][3] // 2}.get(p, 0)
 
 
 def kernel(parts, *refs):
-    args, factors, gathered, late, closing = refs[0:8], *refs[8:12]
+    args, factors, gathered, late_key, late_value, closing = refs[0:8], *refs[8:13]
     (held, share, gain, wide_one, wide_other, box_first, box_next, box_rest, early,
-     load_sem, send_sem, bulk_sem, own_sem, d_sem, box_sem, late_sem, early_sem, row_sem) = refs[12:]
+     load_sem, send_sem, bulk_sem, own_sem, d_sem, box_sem, late_sem, early_sem, row_sem) = refs[13:]
     rows, columns = args[0].shape
     every = range(len(parts))
+    late_rows = late_key.shape[0] + late_value.shape[0]
     base = [sum(part[3] for part in parts[:p]) for p in every]
 
     me = lax.axis_index("rows")
@@ -225,7 +227,6 @@
     def closes(p, j):
         return p == every[-1] and j == parts[p][3] // 2 - 1
 
-    aside = 0
     for p in every:
         chunks = parts[p][3]
         half = chunks // 2
@@ -247,10 +248,9 @@
                 )
                 pltpu.make_async_copy(
                     piece(p, side, j + (1 - core) * half),
-                    late.at[pl.ds(aside, height(p)), :],
+                    (late_value if p == every[-1] else late_key).at[pl.ds(j * height(p), height(p)), :],
                     late_sem,
                 ).start()
-                aside += height(p)
     for p in every:
         half = parts[p][3] // 2
         for j in range(half):
@@ -267,8 +267,8 @@
     sizes = {
         stream: gathered.at[:, pl.ds(0, rows), :] for stream in (OWN_S, X_S, Y_S)
     } | {
-        DIAG: gathered.at[0, pl.ds(0, 3 * rows - late.shape[0]), :],
-        D_S: gathered.at[0, pl.ds(0, 3 * rows - late.shape[0] - closing.shape[0]), :],
+        DIAG: gathered.at[0, pl.ds(0, 3 * rows - late_rows), :],
+        D_S: gathered.at[0, pl.ds(0, 3 * rows - late_rows - closing.shape[0]), :],
     } | {
         stream: gathered.at[pl.ds(0, 2), pl.ds(0, 3 * rows * columns // (2 * width) - height(0)), pl.ds(0, width)]
         for stream in (OWN_X, OWN_Y)
@@ -279,72 +279,74 @@
             moved.wait_recv()
         moved.wait_send()
     early_all.wait_send()
-    pltpu.make_async_copy(gathered.at[0, pl.ds(0, late.shape[0]), :], late, late_sem).wait()
+    put = gathered.at[0, pl.ds(0, late_rows), :]
+    pltpu.make_async_copy(put, put, late_sem).wait()
     for which, box in enumerate((box_first, box_next, box_rest)):
         exchanged(box, which).wait_send()
 
 
-def settle(parts, factors, gathered, *refs):
-    targets, sems = refs[:6], refs[6]
+def writes_of(parts, m, rows, me):
+    p = len(parts) - 3 + m
+    chunks = parts[p][3]
+    height, half, late = rows // chunks, chunks // 2, late_pairs(parts, p)
+    for d in range(8):
+        owner = opposite(me, d)
+        core = lax.rem(owner, 2)
+        if late == 0 or d < 6:
+            yield owner * rows, rows
+        elif late == half:
+            yield owner * rows + core * half * height, (half - 1) * height
+        else:
+            yield owner * rows + core * late * height, half * height
+            yield owner * rows + (half + late) * height, (half - late) * height
+
+
+def write_out(parts, gathered, targets, sems):
     rows = gathered.shape[1] // 8
-    me = lax.axis_index("rows")
     copies = []
-
-    def write(m, at, size):
-        at = pl.multiple_of(at, 16)
-        copies.append(
-            pltpu.make_async_copy(
-                gathered.at[m, pl.ds(at, size), :], targets[m].at[pl.ds(at, size), :], sems.at[len(copies)]
+    for m, target in targets:
+        for at, size in writes_of(parts, m, rows, lax.axis_index("rows")):
+            at = pl.multiple_of(at, 16)
+            copies.append(
+                pltpu.make_async_copy(
+                    gathered.at[m, pl.ds(at, size), :], target.at[pl.ds(at, size), :], sems.at[len(copies)]
+                )
             )
-        )
-
-    for p in range(len(parts) - 3, len(parts)):
-        m, _, _, chunks = parts[p]
-        height, half = rows // chunks, chunks // 2
-        for d in range(8):
-            owner = opposite(me, d)
-            core = lax.rem(owner, 2)
-            late = late_pairs(parts, p)
-            if late == 0 or d < 6:
-                write(m, owner * rows, rows)
-            elif late == half:
-                write(m, owner * rows + core * half * height, (half - 1) * height)
-            else:
-                write(m, owner * rows + core * late * height, half * height)
-                write(m, owner * rows + (half + late) * height, (half - late) * height)
     for c in copies:
         c.start()
+    return copies
+
+
+def settle(parts, factors, gathered, query, key, *refs):
+    copies = write_out(parts, gathered, ((0, query), (1, key)), refs[-1])
     for m in range(3):
-        targets[3 + m][...] = factors[m, 0]
+        refs[m][...] = factors[m, 0]
     for c in copies:
         c.wait()
 
 
-def finish(parts, places, *refs):
+def settle_value(parts, gathered, key, out_key, value, sems):
+    for c in write_out(parts, gathered, ((2, value),), sems):
+        c.wait()
+
+
+def finish(places, *refs):
     given = refs[:len(places)]
     key, value, sems = refs[-3:]
     rows = value.shape[0] // 8
     copies = []
 
-    def write(ref, start, size, out, at):
+    def write(ref, size, out, at):
         at = pl.multiple_of(at, 16)
-        copies.append(
-            pltpu.make_async_copy(
-                ref.at[pl.ds(start, size), :], out.at[pl.ds(at, size), :], sems.at[len(copies)]
-            )
-        )
-
-    for ref, (closing, d) in zip(given, places):
+        copies.append(pltpu.make_async_copy(ref, out.at[pl.ds(at, size), :], sems.at[len(copies)]))
+
+    for ref, (matrix, d) in zip(given, places):
         owner = opposite(lax.axis_index("rows"), d)
-        core = lax.rem(owner, 2)
-        if closing:
-            write(ref, 0, ref.shape[0], value, owner * rows + (1 + core) * (rows // 2) - ref.shape[0])
-            continue
-        start = 0
-        for p, out in ((len(parts) - 2, key), (len(parts) - 1, value)):
-            size = rows // parts[p][3] * late_pairs(parts, p)
-            write(ref, start, size, out, owner * rows + (1 - core) * (rows // 2))
-            start += size
+        core, size = lax.rem(owner, 2), ref.shape[0]
+        if matrix is None:
+            write(ref, size, value, owner * rows + (1 + core) * (rows // 2) - size)
+        else:
+            write(ref, size, (key, value)[matrix - 1], owner * rows + (1 - core) * (rows // 2))
     for c in copies:
         c.start()
     for c in copies:
@@ -354,7 +356,7 @@
 def gathered_by_kernel(*arrays):
     rows, columns = arrays[0].shape
     parts = parts_of(columns)
-    late_rows = sum(rows // part[3] * late_pairs(parts, p) for p, part in enumerate(parts))
+    late_rows = [rows // part[3] * late_pairs(parts, p) for p, part in enumerate(parts)]
     vmem, hbm = pl.BlockSpec(memory_space=pltpu.VMEM), pl.BlockSpec(memory_space=pltpu.HBM)
     anywhere = pl.BlockSpec(memory_space=pl.ANY)
     dma = pltpu.SemaphoreType.DMA
@@ -363,11 +365,12 @@
         out_shape=[
             pltpu.VMEM((3, 1, columns), jnp.float32),
             pltpu.VMEM((3, 8 * rows, columns), jnp.bfloat16),
-            pltpu.VMEM((late_rows, columns), jnp.bfloat16),
+            pltpu.VMEM((late_rows[-2], columns), jnp.bfloat16),
+            pltpu.VMEM((late_rows[-1], columns), jnp.bfloat16),
             pltpu.VMEM((rows // parts[-1][3], columns), jnp.bfloat16),
         ],
         in_specs=[hbm] * 8,
-        out_specs=[vmem] * 4,
+        out_specs=[vmem] * 5,
         scratch_shapes=[
             pltpu.VMEM((6, rows, columns), jnp.float32),
             pltpu.VMEM((rows,), jnp.float32),
@@ -392,47 +395,70 @@
             collective_id=0, has_side_effects=True, vmem_limit_bytes=21 * 2**20
         ),
     )(*arrays)
-    factors, gathered, late, closing = [
+    factors, gathered, late_key, late_value, closing = [
         pltpu.with_memory_space_constraint(r, pltpu.VMEM) for r in results
     ]
     whole = jax.ShapeDtypeStruct((8 * rows, columns), jnp.bfloat16)
+    scales = jax.ShapeDtypeStruct((columns,), jnp.float32)
+    limit = pltpu.CompilerParams(vmem_limit_bytes=2**20)
+
+    def cost(size):
+        return pl.CostEstimate(flops=0, bytes_accessed=size, transcendentals=0)
+
+    across = [(i, i ^ (2, 4)[i % 2]) for i in range(8)]
     siblings = [(i, i ^ 1) for i in range(8)]
-    mine = lax.ppermute(late, "rows", [(i, i ^ (2, 4)[i % 2]) for i in range(8)])
+    value_mine = lax.ppermute(late_value, "rows", across)
+    key_mine = lax.ppermute(late_key, "rows", across)
     closing_other = lax.ppermute(closing, "rows", siblings)
-    query, key, value, *factors = pl.pallas_call(
+    query, key, *factors = pl.pallas_call(
         functools.partial(settle, parts),
-        out_shape=[whole] * 3 + [jax.ShapeDtypeStruct((columns,), jnp.float32)] * 3,
+        out_shape=[whole] * 2 + [scales] * 3,
         in_specs=[vmem] * 2,
-        out_specs=[anywhere] * 3 + [vmem] * 3,
-        scratch_shapes=[dma((26,))],
-        cost_estimate=pl.CostEstimate(flops=0, bytes_accessed=48 * rows * columns, transcendentals=0),
-        compiler_params=pltpu.CompilerParams(vmem_limit_bytes=2**20),
+        out_specs=[anywhere] * 2 + [vmem] * 3,
+        scratch_shapes=[dma((18,))],
+        cost_estimate=cost(32 * rows * columns),
+        compiler_params=limit,
     )(factors, gathered)
-    mine, closing_other, key, value = lax.optimization_barrier((mine, closing_other, key, value))
-    other = lax.ppermute(mine, "rows", siblings)
+    value_mine, closing_other, key = lax.optimization_barrier((value_mine, closing_other, key))
+    value_other = lax.ppermute(value_mine, "rows", siblings)
+    key, value = pl.pallas_call(
+        functools.partial(settle_value, parts),
+        out_shape=[whole] * 2,
+        in_specs=[vmem, anywhere],
+        out_specs=[anywhere] * 2,
+        scratch_shapes=[dma((8,))],
+        input_output_aliases={1: 0},
+        cost_estimate=cost(16 * rows * columns),
+        compiler_params=limit,
+    )(gathered, key)
+    key_mine, value_other, key, value = lax.optimization_barrier((key_mine, value_other, key, value))
+    key_other = lax.ppermute(key_mine, "rows", siblings)
     for places, given in (
-        (((False, 6), (True, 6), (True, 7)), (mine, closing, closing_other)),
-        (((False, 7),), (other,)),
+        (
+            ((2, 6), (1, 6), (None, 6), (None, 7), (2, 7)),
+            (value_mine, key_mine, closing, closing_other, value_other),
+        ),
+        (((1, 7),), (key_other,)),
     ):
         n = len(given)
         key, value = pl.pallas_call(
-            functools.partial(finish, parts, places),
+            functools.partial(finish, places),
             out_shape=[whole] * 2,
             in_specs=[vmem] * n + [anywhere] * 2,
             out_specs=[anywhere] * 2,
-            scratch_shapes=[dma((n + 1,))],
+            scratch_shapes=[dma((n,))],
             input_output_aliases={n: 0, n + 1: 1},
-            cost_estimate=pl.CostEstimate(flops=0, bytes_accessed=4 * late_rows * columns, transcendentals=0),
-            compiler_params=pltpu.CompilerParams(vmem_limit_bytes=2**20),
+            cost_estimate=cost(8 * late_rows[-1] * columns),
+            compiler_params=limit,
         )(*given, key, value)
     return query, key, value, *factors
 
 
 def solution(mesh):
     placed = (P("rows", "model"),) * 6 + (P("rows"),) * 2
-    local = gathered_by_kernel if mesh.shape["rows"] == 8 else gathered_by_collectives
+    relayed = mesh.shape["rows"] == 8
     return jax.shard_map(
-        local,
+        gathered_by_kernel if relayed else gathered_by_collectives,
         mesh=mesh,
         in_specs=placed,
         out_specs=(P(None, "model"),) * 3 + (P("model"),) * 3,

time: 175 us -> 178 us (1.017)
  waiting for transfers between devices: 2.15 us -> 5.88 us
  Pallas kernels: 171 us -> 169 us
    ppermute x2 -> x4, waiting for transfers between devices: 2.15 us -> 5.88 us  [the longest x1 3.46 us: gathered_by_kernel(): key_mine = lax.ppermute(late_key, 'rows', across)]
    pallas_call x1, Pallas kernels: 156 us -> 153 us  [gathered_by_kernel(): pl.pallas_call(functools.partial(kernel, parts), out_shape=[pltpu.VMEM((3...]
    pallas_call x3 -> x4, Pallas kernels: 14.8 us -> 15.6 us  [the longest x1 9.11 us: gathered_by_kernel(): pl.pallas_call(functools.partial(settle, parts), out_shape=[whole] * 2 +...]
  transfers between devices with their start and end apart: 3 -> 5, of which waited for: 2 -> 3; matrix products, arithmetic and copies ran while one was open for 0% -> 0% of each run, Pallas kernels for 8% -> 8%
where the time goes in v3:
time: 178 us
  Pallas kernels  169 us (95%)
  waiting for transfers between devices  5.88 us (3%)
  starting transfers between devices  2.41 us (1%)
    pallas_call x1, Pallas kernels, gathered_by_kernel(): pl.pallas_call(functools.partial(kernel, parts), out_shape=[pltpu.VMEM((3...  153 us
    pallas_call x1, Pallas kernels, gathered_by_kernel(): pl.pallas_call(functools.partial(settle, parts), out_shape=[whole] * 2 +...  9.11 us
    pallas_call x1, Pallas kernels, gathered_by_kernel(): pl.pallas_call(functools.partial(settle_value, parts), out_shape=[whole]...  4.2 us
  transfers between devices with their start and end apart: 5, of which 3 were waited for; matrix products, arithmetic and copies ran while one was open for 0% of the time, Pallas kernels for 8%

profile of v3, /device:TPU:0, one launch (start us, length us, event | category | flops | bytes accessed | tf_op | source)
XLA Modules:
  0.0 177.9 jit_solution(8535448082935906007)
XLA Ops:
  0.6 153.4 %shard_map.127 = (f32[3,1,1280]{2,1,0:T(1,128)S(1)}, bf16[3,5120,1280]{2,1,0:T(8,128)(2,1)S(1)}, bf16[192,1280]{1,0:T(8,128)(2,1)S(1)}, bf16[320,1280]{1,0:T(8,128)(2,1)S(1)}, bf16[64,1280]{1,0:T(8,128)(2,1)S(1)}) custom-call(f32[640,1280]{1,0:T(8,128)} %refs_0_.1, f32[640,1280]{1,0:T(8,128)} %refs_1_.1, f32[640,1280]{1,0:T(8,128)} %refs_2_.1, ...), custom_call_target="tpu_custom_call" | custom-call | tf_op jit(solution)/shard_map/pallas_call | solution.py:363
  154.0 1.2 collective-permute-start.1
  155.3 0.0 collective-permute-start.2
  155.3 9.1 %shard_map.128 = (bf16[5120,1280]{1,0:T(8,128)(2,1)}, bf16[5120,1280]{1,0:T(8,128)(2,1)}, f32[1280]{0:T(1024)}, f32[1280]{0:T(1024)}, f32[1280]{0:T(1024)}) custom-call(f32[3,1,1280]{2,1,0:T(1,128)S(1)} %get-tuple-element.29.factors, bf16[3,5120,1280]{2,1,0:T(8,128)(2,1)S(1)} %get-tuple-element.30.gathered), custom_call_target="tpu_custom_call" | custom-call | bytes 26214400 | tf_op jit(solution)/shard_map/pallas_call | solution.py:413
  164.4 0.0 collective-permute-done.2.refs_3_
  164.4 2.0 %collective-permute-done.1.refs_0_ = bf16[320,1280]{1,0:T(8,128)(2,1)S(1)} collective-permute-done((bf16[320,1280]{1,0:T(8,128)(2,1)S(1)}, bf16[320,1280]{1,0:T(8,128)(2,1)S(1)}, u32[]{:S(2)}, u32[]{:S(2)}) %collective-permute-start.1) | collective-permute-done | bytes 819232 | tf_op jit(solution)/shard_map/ppermute | solution.py:410
  166.4 0.0 collective-permute-start.3
  166.4 1.2 collective-permute-start
  167.6 4.2 %shard_map.129 = (bf16[5120,1280]{1,0:T(8,128)(2,1)}, bf16[5120,1280]{1,0:T(8,128)(2,1)}) custom-call(bf16[3,5120,1280]{2,1,0:T(8,128)(2,1)S(1)} %get-tuple-element.30.gathered, bf16[5120,1280]{1,0:T(8,128)(2,1)} %get-tuple-element.37.key), custom_call_target="tpu_custom_call", output_to_operand_aliasing={{0}: (1, {})} | custom-call | bytes 13107200 | tf_op jit(solution)/shard_map/pallas_call | solution.py:424
  171.8 3.5 %collective-permute-done.refs_1_ = bf16[192,1280]{1,0:T(8,128)(2,1)S(1)} collective-permute-done((bf16[192,1280]{1,0:T(8,128)(2,1)S(1)}, bf16[192,1280]{1,0:T(8,128)(2,1)S(1)}, u32[]{:S(2)}, u32[]{:S(2)}) %collective-permute-start) | collective-permute-done | bytes 491552 | tf_op jit(solution)/shard_map/ppermute | solution.py:411
  175.3 0.0 collective-permute-done.3.refs_4_
  175.3 0.0 collective-permute-start.4
  175.3 1.5 shard_map.130
  176.8 0.4 collective-permute-done.4.refs_0_
  177.1 0.8 shard_map.131
Async XLA Ops:
  154.0 12.4 %collective-permute-start.1 = (bf16[320,1280]{1,0:T(8,128)(2,1)S(1)}, bf16[320,1280]{1,0:T(8,128)(2,1)S(1)}, u32[]{:S(2)}, u32[]{:S(2)}) collective-permute-start(bf16[320,1280]{1,0:T(8,128)(2,1)S(1)} %get-tuple-element.33), channel_id=1, source_target_pairs={{0,8},{4,20},{8,0},{12,28},{16,24},{20,4},{24,16},{28,12},{1,9},{5... | collective-permute-start | bytes 2457608 | tf_op jit(solution)/shard_map/ppermute | solution.py:410
  155.3 9.1 %collective-permute-start.2 = (bf16[64,1280]{1,0:T(8,128)(2,1)S(1)}, bf16[64,1280]{1,0:T(8,128)(2,1)S(1)}, u32[]{:S(2)}, u32[]{:S(2)}) collective-permute-start(bf16[64,1280]{1,0:T(8,128)(2,1)S(1)} %get-tuple-element.34.refs_2_), channel_id=1, source_target_pairs={{0,4},{4,0},{8,12},{12,8},{16,20},{20,16},{24,28},{28,24},{1,5},{5... | collective-permute-start | bytes 491528 | tf_op jit(solution)/shard_map/ppermute | solution.py:412
  166.4 8.8 %collective-permute-start.3 = (bf16[320,1280]{1,0:T(8,128)(2,1)S(1)}, bf16[320,1280]{1,0:T(8,128)(2,1)S(1)}, u32[]{:S(2)}, u32[]{:S(2)}) collective-permute-start(bf16[320,1280]{1,0:T(8,128)(2,1)S(1)} %collective-permute-done.1.refs_0_), channel_id=1, source_target_pairs={{0,4},{4,0},{8,12},{12,8},{16,20},{20,16},{24,28},{28,24},{1,5},{5... | collective-permute-start | bytes 2457608 | tf_op jit(solution)/shard_map/ppermute | solution.py:423
  166.4 8.8 %collective-permute-start = (bf16[192,1280]{1,0:T(8,128)(2,1)S(1)}, bf16[192,1280]{1,0:T(8,128)(2,1)S(1)}, u32[]{:S(2)}, u32[]{:S(2)}) collective-permute-start(bf16[192,1280]{1,0:T(8,128)(2,1)S(1)} %get-tuple-element.32), channel_id=1, source_target_pairs={{0,8},{4,20},{8,0},{12,28},{16,24},{20,4},{24,16},{28,12},{1,9},{5... | collective-permute-start | bytes 1474568 | tf_op jit(solution)/shard_map/ppermute | solution.py:411
  175.3 1.9 %collective-permute-start.4 = (bf16[192,1280]{1,0:T(8,128)(2,1)S(1)}, bf16[192,1280]{1,0:T(8,128)(2,1)S(1)}, u32[]{:S(2)}, u32[]{:S(2)}) collective-permute-start(bf16[192,1280]{1,0:T(8,128)(2,1)S(1)} %collective-permute-done.refs_1_), channel_id=1, source_target_pairs={{0,4},{4,0},{8,12},{12,8},{16,20},{20,16},{24,28},{28,24},{1,5},{5... | collective-permute-start | bytes 1474568 | tf_op jit(solution)/shard_map/ppermute | solution.py:435

commit v4 on v3

--- a/solution.py
+++ b/solution.py
@@ -43,6 +43,13 @@
     )
 
 
+def waits_of(parts):
+    return tuple(
+        (part[3], part[3] // 2) if p == 0 else (2 if part[3] > 2 else 1, 1)
+        for p, part in enumerate(parts)
+    )
+
+
 def late_pairs(parts, p):
     return {len(parts) - 2: 3, len(parts) - 1: parts[p][3] // 2}.get(p, 0)
 
@@ -54,7 +61,17 @@
     rows, columns = args[0].shape
     every = range(len(parts))
     late_rows = late_key.shape[0] + late_value.shape[0]
-    base = [sum(part[3] for part in parts[:p]) for p in every]
+    waits = waits_of(parts)
+    own_base = [sum(q[3] // w[0] for q, w in zip(parts[:p], waits)) for p in every]
+    d_base = [sum(q[3] // 2 // w[1] for q, w in zip(parts[:p], waits)) for p in every]
+    bulk = {OWN_S: 0, X_S: 1, Y_S: 2, D_S: 3}
+
+    def own_arrival(p, k):
+        return own_sem.at[own_base[p] + k // waits[p][0]]
+
+    def d_arrival(p, j):
+        return d_sem.at[d_base[p] + j // waits[p][1]]
+
 
     me = lax.axis_index("rows")
     core = lax.rem(me, 2)
@@ -152,9 +169,9 @@
 
     def send_own(p, k):
         if p or k not in ahead:
-            send(p, me, k, OWN_X, at_x, own_sem.at[base[p] + k])
-            send(p, me, k, OWN_Y, at_y, own_sem.at[base[p] + k])
-        send(p, me, k, OWN_S, sibling, bulk_sem.at[OWN_S])
+            send(p, me, k, OWN_X, at_x, own_arrival(p, k))
+            send(p, me, k, OWN_Y, at_y, own_arrival(p, k))
+        send(p, me, k, OWN_S, sibling, bulk_sem.at[bulk[OWN_S]])
 
     def narrow_and_send(p, factor, sent):
         factors[parts[p][0], :, columns_of(p)] = factor
@@ -231,19 +248,20 @@
         chunks = parts[p][3]
         half = chunks // 2
         for k in range(chunks):
-            if p or k not in ahead:
-                arrived(piece(p, 0, 0, 2), own_sem.at[base[p] + k]).wait_recv()
-            send(p, at_x, k, X_S, sibling, bulk_sem.at[X_S])
-            send(p, at_y, k, Y_S, sibling, bulk_sem.at[Y_S])
+            if k % waits[p][0] == 0:
+                count = waits[p][0] - (0 if p else len(ahead))
+                arrived(piece(p, 0, 0, 2 * count), own_arrival(p, k)).wait_recv()
+            send(p, at_x, k, X_S, sibling, bulk_sem.at[bulk[X_S]])
+            send(p, at_y, k, Y_S, sibling, bulk_sem.at[bulk[Y_S]])
             j = k % half
             if j >= late_pairs(parts, p):
                 if k < half:
-                    send(p, at_x, k, DIAG, at_y, d_sem.at[base[p] // 2 + j])
+                    send(p, at_x, k, DIAG, at_y, d_arrival(p, j))
                 else:
-                    send(p, at_y, k, DIAG, at_x, d_sem.at[base[p] // 2 + j])
+                    send(p, at_y, k, DIAG, at_x, d_arrival(p, j))
             elif k >= half:
                 send(
-                    p, near, j + core * half, DIAG, side, d_sem.at[base[p] // 2 + j],
+                    p, near, j + core * half, DIAG, side, d_arrival(p, j),
                     closing if closes(p, j) else None,
                 )
                 pltpu.make_async_copy(
@@ -255,13 +273,14 @@
         half = parts[p][3] // 2
         for j in range(half):
             if j >= late_pairs(parts, p):
-                arrived(piece(p, 0, 0, 2), d_sem.at[base[p] // 2 + j]).wait_recv()
-                send(p, at_d, j, D_S, sibling, bulk_sem.at[D_S])
-                send(p, at_d, j + half, D_S, sibling, bulk_sem.at[D_S])
+                if j % waits[p][1] == 0:
+                    arrived(piece(p, 0, 0, 2 * waits[p][1]), d_arrival(p, j)).wait_recv()
+                send(p, at_d, j, D_S, sibling, bulk_sem.at[bulk[D_S]])
+                send(p, at_d, j + half, D_S, sibling, bulk_sem.at[bulk[D_S]])
             else:
-                arrived(piece(p, 0, 0, 1), d_sem.at[base[p] // 2 + j]).wait_recv()
+                arrived(piece(p, 0, 0, 1), d_arrival(p, j)).wait_recv()
                 if not closes(p, j):
-                    send(p, at_d, j + core * half, D_S, sibling, bulk_sem.at[D_S])
+                    send(p, at_d, j + core * half, D_S, sibling, bulk_sem.at[bulk[D_S]])
 
     width = parts[0][2]
     sizes = {
@@ -274,8 +293,8 @@
         for stream in (OWN_X, OWN_Y)
     }
     for stream, size in sizes.items():
-        moved = arrived(size, bulk_sem.at[stream], stream)
-        if stream in (OWN_S, X_S, Y_S, D_S):
+        moved = arrived(size, bulk_sem.at[bulk.get(stream, 0)], stream)
+        if stream in bulk:
             moved.wait_recv()
         moved.wait_send()
     early_all.wait_send()
@@ -356,6 +375,7 @@
 def gathered_by_kernel(*arrays):
     rows, columns = arrays[0].shape
     parts = parts_of(columns)
+    waits = waits_of(parts)
     late_rows = [rows // part[3] * late_pairs(parts, p) for p, part in enumerate(parts)]
     vmem, hbm = pl.BlockSpec(memory_space=pltpu.VMEM), pl.BlockSpec(memory_space=pltpu.HBM)
     anywhere = pl.BlockSpec(memory_space=pl.ANY)
@@ -383,9 +403,9 @@
             pltpu.VMEM((2, 2, rows // parts[0][3], parts[0][2]), jnp.float32),
             dma((4,)),
             dma((7,)),
-            dma((7,)),
-            dma((sum(part[3] for part in parts),)),
-            dma((sum(part[3] // 2 for part in parts),)),
+            dma((4,)),
+            dma((sum(part[3] // w[0] for part, w in zip(parts, waits)),)),
+            dma((sum(part[3] // 2 // w[1] for part, w in zip(parts, waits)),)),
             dma((6,)),
             dma(()),
             dma((2,)),

time: 178 us -> 178 us (level)
  no operation moved by 1% of the time
where the time goes in v4:
time: 178 us
  Pallas kernels  169 us (95%)
  waiting for transfers between devices  5.88 us (3%)
  starting transfers between devices  2.41 us (1%)
    pallas_call x1, Pallas kernels, gathered_by_kernel(): pl.pallas_call(functools.partial(kernel, parts), out_shape=[pltpu.VMEM((3...  153 us
    pallas_call x1, Pallas kernels, gathered_by_kernel(): pl.pallas_call(functools.partial(settle, parts), out_shape=[whole] * 2 +...  9.11 us
    pallas_call x1, Pallas kernels, gathered_by_kernel(): pl.pallas_call(functools.partial(settle_value, parts), out_shape=[whole]...  4.2 us
  transfers between devices with their start and end apart: 5, of which 3 were waited for; matrix products, arithmetic and copies ran while one was open for 0% of the time, Pallas kernels for 8%

profile of v4, /device:TPU:0, one launch (start us, length us, event | category | flops | bytes accessed | tf_op | source)
XLA Modules:
  0.0 177.7 jit_solution(4531245745451633212)
XLA Ops:
  0.6 153.2 %shard_map.127 = (f32[3,1,1280]{2,1,0:T(1,128)S(1)}, bf16[3,5120,1280]{2,1,0:T(8,128)(2,1)S(1)}, bf16[192,1280]{1,0:T(8,128)(2,1)S(1)}, bf16[320,1280]{1,0:T(8,128)(2,1)S(1)}, bf16[64,1280]{1,0:T(8,128)(2,1)S(1)}) custom-call(f32[640,1280]{1,0:T(8,128)} %refs_0_.1, f32[640,1280]{1,0:T(8,128)} %refs_1_.1, f32[640,1280]{1,0:T(8,128)} %refs_2_.1, ...), custom_call_target="tpu_custom_call" | custom-call | tf_op jit(solution)/shard_map/pallas_call | solution.py:383
  153.8 1.2 collective-permute-start.1
  155.0 0.0 collective-permute-start.2
  155.0 9.1 %shard_map.128 = (bf16[5120,1280]{1,0:T(8,128)(2,1)}, bf16[5120,1280]{1,0:T(8,128)(2,1)}, f32[1280]{0:T(1024)}, f32[1280]{0:T(1024)}, f32[1280]{0:T(1024)}) custom-call(f32[3,1,1280]{2,1,0:T(1,128)S(1)} %get-tuple-element.29.factors, bf16[3,5120,1280]{2,1,0:T(8,128)(2,1)S(1)} %get-tuple-element.30.gathered), custom_call_target="tpu_custom_call" | custom-call | bytes 26214400 | tf_op jit(solution)/shard_map/pallas_call | solution.py:433
  164.2 0.0 collective-permute-done.2.refs_3_
  164.2 2.0 %collective-permute-done.1.refs_0_ = bf16[320,1280]{1,0:T(8,128)(2,1)S(1)} collective-permute-done((bf16[320,1280]{1,0:T(8,128)(2,1)S(1)}, bf16[320,1280]{1,0:T(8,128)(2,1)S(1)}, u32[]{:S(2)}, u32[]{:S(2)}) %collective-permute-start.1) | collective-permute-done | bytes 819232 | tf_op jit(solution)/shard_map/ppermute | solution.py:430
  166.2 0.0 collective-permute-start.3
  166.2 1.2 collective-permute-start
  167.4 4.2 %shard_map.129 = (bf16[5120,1280]{1,0:T(8,128)(2,1)}, bf16[5120,1280]{1,0:T(8,128)(2,1)}) custom-call(bf16[3,5120,1280]{2,1,0:T(8,128)(2,1)S(1)} %get-tuple-element.30.gathered, bf16[5120,1280]{1,0:T(8,128)(2,1)} %get-tuple-element.37.key), custom_call_target="tpu_custom_call", output_to_operand_aliasing={{0}: (1, {})} | custom-call | bytes 13107200 | tf_op jit(solution)/shard_map/pallas_call | solution.py:444
  171.6 3.5 %collective-permute-done.refs_1_ = bf16[192,1280]{1,0:T(8,128)(2,1)S(1)} collective-permute-done((bf16[192,1280]{1,0:T(8,128)(2,1)S(1)}, bf16[192,1280]{1,0:T(8,128)(2,1)S(1)}, u32[]{:S(2)}, u32[]{:S(2)}) %collective-permute-start) | collective-permute-done | bytes 491552 | tf_op jit(solution)/shard_map/ppermute | solution.py:431
  175.0 0.0 collective-permute-done.3.refs_4_
  175.0 0.0 collective-permute-start.4
  175.1 1.5 shard_map.130
  176.5 0.4 collective-permute-done.4.refs_0_
  176.9 0.8 shard_map.131
Async XLA Ops:
  153.8 12.4 %collective-permute-start.1 = (bf16[320,1280]{1,0:T(8,128)(2,1)S(1)}, bf16[320,1280]{1,0:T(8,128)(2,1)S(1)}, u32[]{:S(2)}, u32[]{:S(2)}) collective-permute-start(bf16[320,1280]{1,0:T(8,128)(2,1)S(1)} %get-tuple-element.33), channel_id=1, source_target_pairs={{0,8},{4,20},{8,0},{12,28},{16,24},{20,4},{24,16},{28,12},{1,9},{5... | collective-permute-start | bytes 2457608 | tf_op jit(solution)/shard_map/ppermute | solution.py:430
  155.0 9.1 %collective-permute-start.2 = (bf16[64,1280]{1,0:T(8,128)(2,1)S(1)}, bf16[64,1280]{1,0:T(8,128)(2,1)S(1)}, u32[]{:S(2)}, u32[]{:S(2)}) collective-permute-start(bf16[64,1280]{1,0:T(8,128)(2,1)S(1)} %get-tuple-element.34.refs_2_), channel_id=1, source_target_pairs={{0,4},{4,0},{8,12},{12,8},{16,20},{20,16},{24,28},{28,24},{1,5},{5... | collective-permute-start | bytes 491528 | tf_op jit(solution)/shard_map/ppermute | solution.py:432
  166.2 8.8 %collective-permute-start.3 = (bf16[320,1280]{1,0:T(8,128)(2,1)S(1)}, bf16[320,1280]{1,0:T(8,128)(2,1)S(1)}, u32[]{:S(2)}, u32[]{:S(2)}) collective-permute-start(bf16[320,1280]{1,0:T(8,128)(2,1)S(1)} %collective-permute-done.1.refs_0_), channel_id=1, source_target_pairs={{0,4},{4,0},{8,12},{12,8},{16,20},{20,16},{24,28},{28,24},{1,5},{5... | collective-permute-start | bytes 2457608 | tf_op jit(solution)/shard_map/ppermute | solution.py:443
  166.2 8.8 %collective-permute-start = (bf16[192,1280]{1,0:T(8,128)(2,1)S(1)}, bf16[192,1280]{1,0:T(8,128)(2,1)S(1)}, u32[]{:S(2)}, u32[]{:S(2)}) collective-permute-start(bf16[192,1280]{1,0:T(8,128)(2,1)S(1)} %get-tuple-element.32), channel_id=1, source_target_pairs={{0,8},{4,20},{8,0},{12,28},{16,24},{20,4},{24,16},{28,12},{1,9},{5... | collective-permute-start | bytes 1474568 | tf_op jit(solution)/shard_map/ppermute | solution.py:431
  175.0 1.9 %collective-permute-start.4 = (bf16[192,1280]{1,0:T(8,128)(2,1)S(1)}, bf16[192,1280]{1,0:T(8,128)(2,1)S(1)}, u32[]{:S(2)}, u32[]{:S(2)}) collective-permute-start(bf16[192,1280]{1,0:T(8,128)(2,1)S(1)} %collective-permute-done.refs_1_), channel_id=1, source_target_pairs={{0,4},{4,0},{8,12},{12,8},{16,20},{20,16},{24,28},{28,24},{1,5},{5... | collective-permute-start | bytes 1474568 | tf_op jit(solution)/shard_map/ppermute | solution.py:455

commit v5 on v4

--- a/solution.py
+++ b/solution.py
@@ -84,19 +84,22 @@
 
     def load(p):
         m = parts[p][0]
-        for i in (2 * m, 2 * m + 1):
-            pltpu.make_async_copy(
-                args[i].at[:, columns_of(p)], held.at[i, :, columns_of(p)], load_sem.at[p]
-            ).start()
+        cuts = 1 if p else 5
+        for cut in range(cuts):
+            at = pl.ds(cut * (rows // cuts), rows // cuts)
+            for i in (2 * m, 2 * m + 1):
+                pltpu.make_async_copy(
+                    args[i].at[at, columns_of(p)], held.at[i, at, columns_of(p)], load_sem.at[p]
+                ).start()
 
     def loaded(p):
         ref = held.at[pl.ds(2 * parts[p][0], 2), :, columns_of(p)]
         pltpu.make_async_copy(ref, ref, load_sem.at[p]).wait()
 
+    load(0)
     by_row = [pltpu.make_async_copy(args[6 + i], to, row_sem.at[i]) for i, to in enumerate((share, gain))]
     for c in by_row:
         c.start()
-    load(0)
 
     barrier = pltpu.get_barrier_semaphore()
     for d in range(1, 8):
@@ -121,7 +124,7 @@
             held[2 * m, at, columns_of(p)] = mixed
             return jnp.maximum(top, jnp.abs(mixed))
 
-        top = lax.fori_loop(0, rows // 8, body, jnp.zeros((8, width), jnp.float32), unroll=4)
+        top = lax.fori_loop(0, rows // 8, body, jnp.zeros((8, width), jnp.float32), unroll=4 if p else 16)
         return jnp.max(top, axis=0, keepdims=True)
 
     def exchange(box, which):

time: 178 us -> 178 us (level)
  no operation moved by 1% of the time
where the time goes in v5:
time: 178 us
  Pallas kernels  169 us (95%)
  waiting for transfers between devices  5.99 us (3%)
  starting transfers between devices  2.3 us (1%)
    pallas_call x1, Pallas kernels, gathered_by_kernel(): pl.pallas_call(functools.partial(kernel, parts), out_shape=[pltpu.VMEM((3...  153 us
    pallas_call x1, Pallas kernels, gathered_by_kernel(): pl.pallas_call(functools.partial(settle, parts), out_shape=[whole] * 2 +...  9.11 us
    pallas_call x1, Pallas kernels, gathered_by_kernel(): pl.pallas_call(functools.partial(settle_value, parts), out_shape=[whole]...  4.2 us
  transfers between devices with their start and end apart: 5, of which 3 were waited for; matrix products, arithmetic and copies ran while one was open for 0% of the time, Pallas kernels for 8%

profile of v5, /device:TPU:0, one launch (start us, length us, event | category | flops | bytes accessed | tf_op | source)
XLA Modules:
  0.0 177.8 jit_solution(2387591926470753954)
XLA Ops:
  0.6 153.2 %shard_map.127 = (f32[3,1,1280]{2,1,0:T(1,128)S(1)}, bf16[3,5120,1280]{2,1,0:T(8,128)(2,1)S(1)}, bf16[192,1280]{1,0:T(8,128)(2,1)S(1)}, bf16[320,1280]{1,0:T(8,128)(2,1)S(1)}, bf16[64,1280]{1,0:T(8,128)(2,1)S(1)}) custom-call(f32[640,1280]{1,0:T(8,128)} %refs_0_.1, f32[640,1280]{1,0:T(8,128)} %refs_1_.1, f32[640,1280]{1,0:T(8,128)} %refs_2_.1, ...), custom_call_target="tpu_custom_call" | custom-call | tf_op jit(solution)/shard_map/pallas_call | solution.py:386
  153.9 1.2 collective-permute-start.1
  155.0 0.0 collective-permute-start.2
  155.0 9.1 %shard_map.128 = (bf16[5120,1280]{1,0:T(8,128)(2,1)}, bf16[5120,1280]{1,0:T(8,128)(2,1)}, f32[1280]{0:T(1024)}, f32[1280]{0:T(1024)}, f32[1280]{0:T(1024)}) custom-call(f32[3,1,1280]{2,1,0:T(1,128)S(1)} %get-tuple-element.29.factors, bf16[3,5120,1280]{2,1,0:T(8,128)(2,1)S(1)} %get-tuple-element.30.gathered), custom_call_target="tpu_custom_call" | custom-call | bytes 26214400 | tf_op jit(solution)/shard_map/pallas_call | solution.py:436
  164.2 0.0 collective-permute-done.2.refs_3_
  164.2 2.1 %collective-permute-done.1.refs_0_ = bf16[320,1280]{1,0:T(8,128)(2,1)S(1)} collective-permute-done((bf16[320,1280]{1,0:T(8,128)(2,1)S(1)}, bf16[320,1280]{1,0:T(8,128)(2,1)S(1)}, u32[]{:S(2)}, u32[]{:S(2)}) %collective-permute-start.1) | collective-permute-done | bytes 819232 | tf_op jit(solution)/shard_map/ppermute | solution.py:433
  166.3 0.0 collective-permute-start.3
  166.3 1.1 collective-permute-start
  167.4 4.2 %shard_map.129 = (bf16[5120,1280]{1,0:T(8,128)(2,1)}, bf16[5120,1280]{1,0:T(8,128)(2,1)}) custom-call(bf16[3,5120,1280]{2,1,0:T(8,128)(2,1)S(1)} %get-tuple-element.30.gathered, bf16[5120,1280]{1,0:T(8,128)(2,1)} %get-tuple-element.37.key), custom_call_target="tpu_custom_call", output_to_operand_aliasing={{0}: (1, {})} | custom-call | bytes 13107200 | tf_op jit(solution)/shard_map/pallas_call | solution.py:447
  171.6 3.5 %collective-permute-done.refs_1_ = bf16[192,1280]{1,0:T(8,128)(2,1)S(1)} collective-permute-done((bf16[192,1280]{1,0:T(8,128)(2,1)S(1)}, bf16[192,1280]{1,0:T(8,128)(2,1)S(1)}, u32[]{:S(2)}, u32[]{:S(2)}) %collective-permute-start) | collective-permute-done | bytes 491552 | tf_op jit(solution)/shard_map/ppermute | solution.py:434
  175.1 0.0 collective-permute-done.3.refs_4_
  175.1 0.0 collective-permute-start.4
  175.1 1.5 shard_map.130
  176.6 0.4 collective-permute-done.4.refs_0_
  177.0 0.8 shard_map.131
Async XLA Ops:
  153.9 12.4 %collective-permute-start.1 = (bf16[320,1280]{1,0:T(8,128)(2,1)S(1)}, bf16[320,1280]{1,0:T(8,128)(2,1)S(1)}, u32[]{:S(2)}, u32[]{:S(2)}) collective-permute-start(bf16[320,1280]{1,0:T(8,128)(2,1)S(1)} %get-tuple-element.33), channel_id=1, source_target_pairs={{0,8},{4,20},{8,0},{12,28},{16,24},{20,4},{24,16},{28,12},{1,9},{5... | collective-permute-start | bytes 2457608 | tf_op jit(solution)/shard_map/ppermute | solution.py:433
  155.0 9.1 %collective-permute-start.2 = (bf16[64,1280]{1,0:T(8,128)(2,1)S(1)}, bf16[64,1280]{1,0:T(8,128)(2,1)S(1)}, u32[]{:S(2)}, u32[]{:S(2)}) collective-permute-start(bf16[64,1280]{1,0:T(8,128)(2,1)S(1)} %get-tuple-element.34.refs_2_), channel_id=1, source_target_pairs={{0,4},{4,0},{8,12},{12,8},{16,20},{20,16},{24,28},{28,24},{1,5},{5... | collective-permute-start | bytes 491528 | tf_op jit(solution)/shard_map/ppermute | solution.py:435
  166.3 8.8 %collective-permute-start.3 = (bf16[320,1280]{1,0:T(8,128)(2,1)S(1)}, bf16[320,1280]{1,0:T(8,128)(2,1)S(1)}, u32[]{:S(2)}, u32[]{:S(2)}) collective-permute-start(bf16[320,1280]{1,0:T(8,128)(2,1)S(1)} %collective-permute-done.1.refs_0_), channel_id=1, source_target_pairs={{0,4},{4,0},{8,12},{12,8},{16,20},{20,16},{24,28},{28,24},{1,5},{5... | collective-permute-start | bytes 2457608 | tf_op jit(solution)/shard_map/ppermute | solution.py:446
  166.3 8.8 %collective-permute-start = (bf16[192,1280]{1,0:T(8,128)(2,1)S(1)}, bf16[192,1280]{1,0:T(8,128)(2,1)S(1)}, u32[]{:S(2)}, u32[]{:S(2)}) collective-permute-start(bf16[192,1280]{1,0:T(8,128)(2,1)S(1)} %get-tuple-element.32), channel_id=1, source_target_pairs={{0,8},{4,20},{8,0},{12,28},{16,24},{20,4},{24,16},{28,12},{1,9},{5... | collective-permute-start | bytes 1474568 | tf_op jit(solution)/shard_map/ppermute | solution.py:434
  175.1 1.9 %collective-permute-start.4 = (bf16[192,1280]{1,0:T(8,128)(2,1)S(1)}, bf16[192,1280]{1,0:T(8,128)(2,1)S(1)}, u32[]{:S(2)}, u32[]{:S(2)}) collective-permute-start(bf16[192,1280]{1,0:T(8,128)(2,1)S(1)} %collective-permute-done.refs_1_), channel_id=1, source_target_pairs={{0,4},{4,0},{8,12},{12,8},{16,20},{20,16},{24,28},{28,24},{1,5},{5... | collective-permute-start | bytes 1474568 | tf_op jit(solution)/shard_map/ppermute | solution.py:458
